TPU v7x, 32 devices: a whole 2x2x4 slice. The times are simulated.
32 devices in a mesh: row: 8 (over z, y), col: 4 (over x, core).
Axes of the slice: x: 2, y: 2, z: 4, core: 2. Of those that a mesh axis runs over, the one named last changes fastest.
Arguments:
- matrix_tiles: bfloat16 [8, 4, 96, 256, 256], P('row', 'col'), may hold values from -0.078125 to 0.078125
- tile_rows: int32 [8, 4, 96], P('row', 'col'), may hold values from 0 to 7, as said below
- tile_cols: int32 [8, 4, 96], P('row', 'col'), may hold values from 0 to 15
- tile_count: int32 [8, 4], P('row', 'col'), may hold values from 24 to 96, as said below
- x_start: float32 [16384, 256], P(('col', 'row')), may hold values from -5 to 5
- y_start: float32 [16384, 256], P(('row', 'col')), may hold values from 0 to 1
- cost_vector: float32 [16384, 256], P(('col', 'row')), may hold values from -6 to 6
- right_side: float32 [16384, 256], P(('row', 'col')), may hold values from -6 to 6
- lower_bound: float32 [16384, 256], P(('col', 'row')), may hold values from -1.5 to -0.3
- upper_bound: float32 [16384, 256], P(('col', 'row')), may hold values from 0.3 to 1.5
- step_primal: float32 [256], replicated, may hold values from 0.2 to 0.45
- step_dual: float32 [256], replicated, may hold values from 0.2 to 0.45
Outputs:
- primal_out: float32 [16384, 256], P(('col', 'row'))
- dual_out: float32 [16384, 256], P(('row', 'col'))
Inputs may be any that keep to these rules, and one draw needn't show every extreme that they name: Within one grid cell the pairs (tile_rows, tile_cols) of its slots are all different. `tile_count`: some grid cell has 96 used slots in every draw; slots at or above a cell's count are not part of A.
All inputs are finite; a program needn't handle non-finite values.
Results may differ from a plain program's by a relative error of at most 0.001.
Values may be sent and summed in bfloat16 or wider, within the bound.
A program may use at most 128 MiB of HBM per device.

v0:
```python
import jax
import jax.numpy as jnp
from jax import lax
from jax.sharding import PartitionSpec as P

NR_DEV = 8
SLOT_BLOCK = 16
eps = 1e-06


def forward_part(my_tiles, my_rows, my_cols, slot_count, segment):
    edge = my_tiles.shape[-1]
    batch_width = segment.shape[-1]
    x_tiles = segment.reshape(-1, edge, batch_width)
    slot_ids = jnp.arange(SLOT_BLOCK, dtype=jnp.int32)

    def forward_block_step(block_index, running):
        first_slot = block_index * SLOT_BLOCK
        tile_block = lax.dynamic_slice_in_dim(my_tiles, first_slot, SLOT_BLOCK, 0)
        row_block = lax.dynamic_slice_in_dim(my_rows, first_slot, SLOT_BLOCK, 0)
        col_block = lax.dynamic_slice_in_dim(my_cols, first_slot, SLOT_BLOCK, 0)
        in_use = first_slot + slot_ids < slot_count
        pieces = jnp.take(x_tiles, col_block, axis=0)
        products = jnp.einsum(
            "sij,sjb->sib", tile_block, pieces, preferred_element_type=jnp.float32
        )
        products = jnp.where(in_use[:, None, None], products, jnp.zeros_like(products))
        return running.at[row_block].add(products)

    blocks = (slot_count + SLOT_BLOCK - 1) // SLOT_BLOCK
    begin = jnp.zeros((NR_DEV, edge, batch_width), jnp.float32)
    return lax.fori_loop(0, blocks, forward_block_step, begin).reshape(-1, batch_width)


def backward_part(my_tiles, my_rows, my_cols, slot_count, segment, col_tiles):
    edge = my_tiles.shape[-1]
    batch_width = segment.shape[-1]
    y_tiles = segment.reshape(-1, edge, batch_width)
    slot_ids = jnp.arange(SLOT_BLOCK, dtype=jnp.int32)

    def backward_block_step(block_index, running):
        first_slot = block_index * SLOT_BLOCK
        tile_block = lax.dynamic_slice_in_dim(my_tiles, first_slot, SLOT_BLOCK, 0)
        row_block = lax.dynamic_slice_in_dim(my_rows, first_slot, SLOT_BLOCK, 0)
        col_block = lax.dynamic_slice_in_dim(my_cols, first_slot, SLOT_BLOCK, 0)
        in_use = first_slot + slot_ids < slot_count
        pieces = jnp.take(y_tiles, row_block, axis=0)
        products = jnp.einsum(
            "sij,sib->sjb", tile_block, pieces, preferred_element_type=jnp.float32
        )
        products = jnp.where(in_use[:, None, None], products, jnp.zeros_like(products))
        return running.at[col_block].add(products)

    blocks = (slot_count + SLOT_BLOCK - 1) // SLOT_BLOCK
    begin = jnp.zeros((col_tiles, edge, batch_width), jnp.float32)
    return lax.fori_loop(0, blocks, backward_block_step, begin).reshape(-1, batch_width)


def body(
    matrix_tiles,
    tile_rows,
    tile_cols,
    tile_count,
    x_start,
    y_start,
    cost_vector,
    right_side,
    lower_bound,
    upper_bound,
    step_primal,
    step_dual,
):
    my_tiles = matrix_tiles[0, 0]
    my_rows = tile_rows[0, 0]
    my_cols = tile_cols[0, 0]
    slot_count = tile_count[0, 0]
    row_devices = lax.axis_size("row")
    col_devices = lax.axis_size("col")
    share = x_start.shape[0]
    edge = my_tiles.shape[-1]
    col_tiles = share * row_devices // edge
    total_cols = share * row_devices * col_devices
    total_rows = y_start.shape[0] * row_devices * col_devices

    def dual_rows(values):
        return lax.all_gather(values.astype(jnp.bfloat16), "col", axis=0, tiled=True)

    def row_sums(segment):
        return lax.psum_scatter(
            forward_part(my_tiles, my_rows, my_cols, slot_count, segment),
            "col",
            scatter_dimension=0,
            tiled=True,
        )

    x_base, cost_seg, lower_seg, upper_seg = (x_start, cost_vector, lower_bound, upper_bound)

    def column_sums(segment):
        partial_value = backward_part(my_tiles, my_rows, my_cols, slot_count, segment, col_tiles)
        return lax.psum_scatter(partial_value, "row", scatter_dimension=0, tiled=True)

    def spread(ahead):
        return lax.all_gather(ahead, "row", axis=0, tiled=True)

    grad_zero = column_sums(dual_rows(y_start))
    primal_one = jnp.clip(x_base - step_primal * (cost_seg - grad_zero), lower_seg, upper_seg)
    primal_diff = primal_one - x_base
    move_primal = jnp.sum(primal_diff * primal_diff, axis=0)
    image_one = row_sums(spread((2.0 * primal_one - x_base).astype(jnp.bfloat16)))
    dual_one = jnp.maximum(y_start + step_dual * (right_side - image_one), 0.0)
    dual_diff = dual_one - y_start
    move_dual = jnp.sum(dual_diff * dual_diff, axis=0)
    move_primal, move_dual = lax.psum((move_primal, move_dual), ("row", "col"))
    weight = jnp.sqrt((move_dual / total_rows + eps) / (move_primal / total_cols + eps))
    grad_one = column_sums(dual_rows(dual_one))
    primal_two = jnp.clip(
        primal_one - step_primal / weight * (cost_seg - grad_one), lower_seg, upper_seg
    )
    image_two = row_sums(spread((2.0 * primal_two - primal_one).astype(jnp.bfloat16)))
    dual_out = jnp.maximum(dual_one + step_dual * weight * (right_side - image_two), 0.0)
    return (primal_two, dual_out)


def solution(mesh):
    placed = (
        P("row", "col", None, None, None),
        P("row", "col", None),
        P("row", "col", None),
        P("row", "col"),
        P(("col", "row"), None),
        P(("row", "col"), None),
        P(("col", "row"), None),
        P(("row", "col"), None),
        P(("col", "row"), None),
        P(("col", "row"), None),
        P(),
        P(),
    )
    return jax.shard_map(
        body,
        mesh=mesh,
        in_specs=placed,
        out_specs=(P(("col", "row"), None), P(("row", "col"), None)),
        check_vma=False,
    )
```

profile of v0, /device:TPU:0, one launch (start us, length us, event | category | flops | bytes accessed | tf_op | source)
XLA Modules:
  0.0 772.5 jit_solution(1718431034138353426)
XLA Ops:
  9.7 16.6 %copy.14 = bf16[96,256,256]{1,2,0:T(8,128)(2,1)} copy(bf16[96,256,256]{2,1,0:T(8,128)(2,1)} %bitcast.19) | data formatting | bytes 25165824
  31.9 91.8 %while.44 = (s32[]{:T(128)}, f32[16,256,256]{2,1,0:T(8,128)}, s32[]{:T(128)}, s32[96]{0:T(128)S(1)}, s32[]{:T(128)}, /*index=5*/bf16[96,256,256]{1,2,0:T(8,128)(...) while((s32[]{:T(128)}, f32[16,256,256]{2,1,0:T(8,128)}, ...), condition=%wide.region_2.4_spmd.clone, body=%wide.region_0.3_spmd.clone.sunk | while | flops 540017856 | bytes 25170616 | solution.py:56
  37.8 9.5 %scatter_fusion = f32[16,256,256]{2,1,0:T(8,128)} fusion(f32[16,256,256]{2,1,0:T(8,128)} %get-tuple-element.615, s32[16]{0:T(128)S(1)} %compare_select_fusion.16, f32[16,256,256]{2,1,0:T(8,128)} %convolution_select_fusion.8), kind=kCustom, calls=%fused_computation.4.clone.clone.1 | custom fusion | flops 1048576 | bytes 12582976 | tf_op jit(solution)/shard_map/while/body/scatter-add | solution.py:52
  53.2 9.5 %scatter_fusion = f32[16,256,256]{2,1,0:T(8,128)} fusion(f32[16,256,256]{2,1,0:T(8,128)} %get-tuple-element.615, s32[16]{0:T(128)S(1)} %compare_select_fusion.16, f32[16,256,256]{2,1,0:T(8,128)} %convolution_select_fusion.8), kind=kCustom, calls=%fused_computation.4.clone.clone.1 | custom fusion | flops 1048576 | bytes 12582976 | tf_op jit(solution)/shard_map/while/body/scatter-add | solution.py:52
  68.5 9.5 %scatter_fusion = f32[16,256,256]{2,1,0:T(8,128)} fusion(f32[16,256,256]{2,1,0:T(8,128)} %get-tuple-element.615, s32[16]{0:T(128)S(1)} %compare_select_fusion.16, f32[16,256,256]{2,1,0:T(8,128)} %convolution_select_fusion.8), kind=kCustom, calls=%fused_computation.4.clone.clone.1 | custom fusion | flops 1048576 | bytes 12582976 | tf_op jit(solution)/shard_map/while/body/scatter-add | solution.py:52
  83.8 9.5 %scatter_fusion = f32[16,256,256]{2,1,0:T(8,128)} fusion(f32[16,256,256]{2,1,0:T(8,128)} %get-tuple-element.615, s32[16]{0:T(128)S(1)} %compare_select_fusion.16, f32[16,256,256]{2,1,0:T(8,128)} %convolution_select_fusion.8), kind=kCustom, calls=%fused_computation.4.clone.clone.1 | custom fusion | flops 1048576 | bytes 12582976 | tf_op jit(solution)/shard_map/while/body/scatter-add | solution.py:52
  99.2 9.3 %scatter_fusion = f32[16,256,256]{2,1,0:T(8,128)} fusion(f32[16,256,256]{2,1,0:T(8,128)} %get-tuple-element.615, s32[16]{0:T(128)S(1)} %compare_select_fusion.16, f32[16,256,256]{2,1,0:T(8,128)} %convolution_select_fusion.8), kind=kCustom, calls=%fused_computation.4.clone.clone.1 | custom fusion | flops 1048576 | bytes 12582976 | tf_op jit(solution)/shard_map/while/body/scatter-add | solution.py:52
  114.3 9.5 %scatter_fusion = f32[16,256,256]{2,1,0:T(8,128)} fusion(f32[16,256,256]{2,1,0:T(8,128)} %get-tuple-element.615, s32[16]{0:T(128)S(1)} %compare_select_fusion.16, f32[16,256,256]{2,1,0:T(8,128)} %convolution_select_fusion.8), kind=kCustom, calls=%fused_computation.4.clone.clone.1 | custom fusion | flops 1048576 | bytes 12582976 | tf_op jit(solution)/shard_map/while/body/scatter-add | solution.py:52
  123.8 86.9 %reduce-scatter.5.cloned.1.call-done = f32[512,256]{1,0:T(8,128)} async-done(((f32[4096,256]{1,0:T(8,128)}), f32[512,256]{1,0:T(8,128)}) %reduce-scatter.5.cloned.1.call-update) | async-done | bytes 524304 | tf_op jit(solution)/shard_map/reduce_scatter | solution.py:100
  213.6 48.8 %all-gather.7.cloned.1.call-done = bf16[4096,256]{1,0:T(8,128)(2,1)} async-done(((bf16[512,256]{1,0:T(8,128)(2,1)}), bf16[4096,256]{1,0:T(8,128)(2,1)}) %all-gather.7.cloned.1.call-update) | async-done | bytes 2097168 | tf_op jit(solution)/shard_map/all_gather | solution.py:103
  262.6 93.1 %while.45 = (s32[]{:T(128)}, f32[8,256,256]{2,1,0:T(8,128)S(1)}, s32[]{:T(128)}, s32[96]{0:T(128)S(1)}, s32[]{:T(128)}, /*index=5*/bf16[96,256,256]{2,1,0:T(8,12...) while((s32[]{:T(128)}, f32[8,256,256]{2,1,0:T(8,128)S(1)}, ...), condition=%wide.region_6.9_spmd.clone, body=%wide.region_4.8_spmd.clone.sunk | while | flops 540017856 | bytes 25170616 | solution.py:32
  287.5 6.2 scatter_fusion.1
  303.0 6.1 scatter_fusion.1
  318.5 6.2 scatter_fusion.1
  349.5 6.2 scatter_fusion.1
  357.1 28.9 %reduce-scatter.7.cloned.1.call-done = f32[512,256]{1,0:T(8,128)} async-done(((f32[2048,256]{1,0:T(8,128)}), f32[512,256]{1,0:T(8,128)}) %reduce-scatter.7.cloned.1.call-update) | async-done | bytes 524304 | tf_op jit(solution)/shard_map/reduce_scatter | solution.py:89
  388.8 16.8 %all-gather.9.cloned.1.call-done = bf16[2048,256]{1,0:T(8,128)(2,1)} async-done(((bf16[512,256]{1,0:T(8,128)(2,1)}), bf16[2048,256]{1,0:T(8,128)(2,1)}) %all-gather.9.cloned.1.call-update) | async-done | bytes 1048592 | tf_op jit(solution)/shard_map/all_gather | solution.py:86
  408.0 91.8 %while.46 = (s32[]{:T(128)}, f32[16,256,256]{2,1,0:T(8,128)}, s32[]{:T(128)}, s32[96]{0:T(128)S(1)}, s32[]{:T(128)}, /*index=5*/bf16[96,256,256]{1,2,0:T(8,128)(...) while((s32[]{:T(128)}, f32[16,256,256]{2,1,0:T(8,128)}, ...), condition=%wide.region_14.17_spmd.clone, body=%wide.region_12.16_spmd.clone.sunk | while | flops 540017856 | bytes 25170616 | solution.py:56
  413.8 9.5 %scatter_fusion.2 = f32[16,256,256]{2,1,0:T(8,128)} fusion(f32[16,256,256]{2,1,0:T(8,128)} %get-tuple-element.687, s32[16]{0:T(128)S(1)} %compare_select_fusion.18, f32[16,256,256]{2,1,0:T(8,128)} %convolution_select_fusion.10), kind=kCustom, calls=%fused_computation.6.clone.clone.1 | custom fusion | flops 1048576 | bytes 12582976 | tf_op jit(solution)/shard_map/while/body/scatter-add | solution.py:52
  429.2 9.5 %scatter_fusion.2 = f32[16,256,256]{2,1,0:T(8,128)} fusion(f32[16,256,256]{2,1,0:T(8,128)} %get-tuple-element.687, s32[16]{0:T(128)S(1)} %compare_select_fusion.18, f32[16,256,256]{2,1,0:T(8,128)} %convolution_select_fusion.10), kind=kCustom, calls=%fused_computation.6.clone.clone.1 | custom fusion | flops 1048576 | bytes 12582976 | tf_op jit(solution)/shard_map/while/body/scatter-add | solution.py:52
  444.5 9.5 %scatter_fusion.2 = f32[16,256,256]{2,1,0:T(8,128)} fusion(f32[16,256,256]{2,1,0:T(8,128)} %get-tuple-element.687, s32[16]{0:T(128)S(1)} %compare_select_fusion.18, f32[16,256,256]{2,1,0:T(8,128)} %convolution_select_fusion.10), kind=kCustom, calls=%fused_computation.6.clone.clone.1 | custom fusion | flops 1048576 | bytes 12582976 | tf_op jit(solution)/shard_map/while/body/scatter-add | solution.py:52
  459.8 9.5 %scatter_fusion.2 = f32[16,256,256]{2,1,0:T(8,128)} fusion(f32[16,256,256]{2,1,0:T(8,128)} %get-tuple-element.687, s32[16]{0:T(128)S(1)} %compare_select_fusion.18, f32[16,256,256]{2,1,0:T(8,128)} %convolution_select_fusion.10), kind=kCustom, calls=%fused_computation.6.clone.clone.1 | custom fusion | flops 1048576 | bytes 12582976 | tf_op jit(solution)/shard_map/while/body/scatter-add | solution.py:52
  475.1 9.4 %scatter_fusion.2 = f32[16,256,256]{2,1,0:T(8,128)} fusion(f32[16,256,256]{2,1,0:T(8,128)} %get-tuple-element.687, s32[16]{0:T(128)S(1)} %compare_select_fusion.18, f32[16,256,256]{2,1,0:T(8,128)} %convolution_select_fusion.10), kind=kCustom, calls=%fused_computation.6.clone.clone.1 | custom fusion | flops 1048576 | bytes 12582976 | tf_op jit(solution)/shard_map/while/body/scatter-add | solution.py:52
  490.3 9.4 %scatter_fusion.2 = f32[16,256,256]{2,1,0:T(8,128)} fusion(f32[16,256,256]{2,1,0:T(8,128)} %get-tuple-element.687, s32[16]{0:T(128)S(1)} %compare_select_fusion.18, f32[16,256,256]{2,1,0:T(8,128)} %convolution_select_fusion.10), kind=kCustom, calls=%fused_computation.6.clone.clone.1 | custom fusion | flops 1048576 | bytes 12582976 | tf_op jit(solution)/shard_map/while/body/scatter-add | solution.py:52
  499.8 40.9 %all-reduce = (f32[256]{0:T(256)S(1)}, f32[256]{0:T(256)S(1)}) all-reduce(f32[256]{0:T(256)S(1)} %get-tuple-element.372, f32[256]{0:T(256)S(1)} %get-tuple-element.370), channel_id=1, replica_groups=mesh['row'=8,'col'=4] {'row','col'}, use_global_device_ids=true, to_apply=%region_11.14 | all-reduce | flops 512 | bytes 4096 | tf_op jit(solution)/shard_map/psum | solution.py:113
  540.8 47.3 %reduce-scatter.9.cloned.1.call-done = f32[512,256]{1,0:T(8,128)} async-done(((f32[4096,256]{1,0:T(8,128)}), f32[512,256]{1,0:T(8,128)}) %reduce-scatter.9.cloned.1.call-update) | async-done | bytes 524304 | tf_op jit(solution)/shard_map/reduce_scatter | solution.py:100
  590.2 49.3 %all-gather.11.cloned.1.call-done = bf16[4096,256]{1,0:T(8,128)(2,1)} async-done(((bf16[512,256]{1,0:T(8,128)(2,1)}), bf16[4096,256]{1,0:T(8,128)(2,1)}) %all-gather.11.cloned.1.call-update) | async-done | bytes 2097168 | tf_op jit(solution)/shard_map/all_gather | solution.py:103
  639.7 93.7 %while.47 = (s32[]{:T(128)}, f32[8,256,256]{2,1,0:T(8,128)S(1)}, s32[]{:T(128)}, s32[96]{0:T(128)S(1)}, s32[]{:T(128)}, /*index=5*/bf16[96,256,256]{2,1,0:T(8,12...) while((s32[]{:T(128)}, f32[8,256,256]{2,1,0:T(8,128)S(1)}, ...), condition=%wide.region_18.21_spmd.clone, body=%wide.region_16.20_spmd.clone.sunk | while | flops 540017856 | bytes 25170616 | solution.py:32
  664.7 6.2 scatter_fusion.3
  696.0 6.2 scatter_fusion.3
  727.2 6.2 scatter_fusion.3
  734.8 28.9 %reduce-scatter.11.cloned.1.call-done = f32[512,256]{1,0:T(8,128)} async-done(((f32[2048,256]{1,0:T(8,128)}), f32[512,256]{1,0:T(8,128)}) %reduce-scatter.11.cloned.1.call-update) | async-done | bytes 524304 | tf_op jit(solution)/shard_map/reduce_scatter | solution.py:89
  (199 shorter events, 235.7 us)
Async XLA Ops:
  7.2 22.4 %all-gather.5.cloned.1.call-start = ((), (), s32[]{:S(2)}) async-start(), calls=%async_computation.4 | async-start | bytes 1310720 | tf_op jit(solution)/shard_map/all_gather | solution.py:86
  9.0 201.7 %reduce-scatter.5.cloned.1.call-start = ((), (), s32[]{:S(2)}) async-start(), calls=%async_computation.5 | async-start | bytes 4718592 | tf_op jit(solution)/shard_map/reduce_scatter | solution.py:100
  29.6 2.4 copy-start.2
  29.6 2.4 copy-start.18
  29.6 2.4 copy-start.19
  123.7 87.0 %copy-start.9 = (f32[512,256]{1,0:T(8,128)S(1)}, f32[512,256]{1,0:T(8,128)}, u32[]{:S(2)}) copy-start(f32[512,256]{1,0:T(8,128)} %param.33) | copy-start | bytes 1572868
  123.7 87.0 %copy-start.11 = (f32[512,256]{1,0:T(8,128)S(1)}, f32[512,256]{1,0:T(8,128)}, u32[]{:S(2)}) copy-start(f32[512,256]{1,0:T(8,128)} %param.32) | copy-start | bytes 1572868
  123.7 87.0 %copy-start.13 = (f32[512,256]{1,0:T(8,128)S(1)}, f32[512,256]{1,0:T(8,128)}, u32[]{:S(2)}) copy-start(f32[512,256]{1,0:T(8,128)} %param.30) | copy-start | bytes 1572868
  123.7 87.0 %copy-start.17 = (f32[512,256]{1,0:T(8,128)S(1)}, f32[512,256]{1,0:T(8,128)}, u32[]{:S(2)}) copy-start(f32[512,256]{1,0:T(8,128)} %param.28) | copy-start | bytes 1572868
  123.8 87.0 %copy-start.21 = (f32[256]{0:T(256)S(1)}, f32[256]{0:T(256)}, u32[]{:S(2)}) copy-start(f32[256]{0:T(256)} %param.34) | copy-start | bytes 3076
  123.8 138.6 %all-gather.7.cloned.1.call-start = ((), (), s32[]{:S(2)}) async-start(), calls=%async_computation.6 | async-start | bytes 2359296 | tf_op jit(solution)/shard_map/all_gather | solution.py:103
  211.9 0.8 copy-start.6
  213.5 172.5 %reduce-scatter.7.cloned.1.call-start = ((), (), s32[]{:S(2)}) async-start(), calls=%async_computation.7 | async-start | bytes 2621440 | tf_op jit(solution)/shard_map/reduce_scatter | solution.py:89
  355.7 1.3 copy-start.1
  355.7 30.3 %copy-start.8 = (f32[512,256]{1,0:T(8,128)S(1)}, f32[512,256]{1,0:T(8,128)}, u32[]{:S(2)}) copy-start(f32[512,256]{1,0:T(8,128)} %param.29) | copy-start | bytes 1572868
  355.7 30.2 %copy-start.15 = (f32[512,256]{1,0:T(8,128)S(1)}, f32[512,256]{1,0:T(8,128)}, u32[]{:S(2)}) copy-start(f32[512,256]{1,0:T(8,128)} %param.31) | copy-start | bytes 1572868
  355.8 30.2 %copy-start.20 = (f32[256]{0:T(256)S(1)}, f32[256]{0:T(256)}, u32[]{:S(2)}) copy-start(f32[256]{0:T(256)} %param.35) | copy-start | bytes 3076
  357.1 48.6 %all-gather.9.cloned.1.call-start = ((), (), s32[]{:S(2)}) async-start(), calls=%async_computation.8 | async-start | bytes 1310720 | tf_op jit(solution)/shard_map/all_gather | solution.py:86
  387.2 0.8 copy-start.4
  388.7 199.3 %reduce-scatter.9.cloned.1.call-start = ((), (), s32[]{:S(2)}) async-start(), calls=%async_computation.9 | async-start | bytes 4718592 | tf_op jit(solution)/shard_map/reduce_scatter | solution.py:100
  405.6 2.4 copy-start.3
  499.8 88.3 %copy-start.7 = (f32[512,256]{1,0:T(8,128)S(1)}, f32[512,256]{1,0:T(8,128)}, u32[]{:S(2)}) copy-start(f32[512,256]{1,0:T(8,128)} %copy-done.6) | copy-start | bytes 1572868
  499.8 88.3 %copy-start.10 = (f32[512,256]{1,0:T(8,128)S(1)}, f32[512,256]{1,0:T(8,128)}, u32[]{:S(2)}) copy-start(f32[512,256]{1,0:T(8,128)} %param.33) | copy-start | bytes 1572868
  499.8 88.3 %copy-start.12 = (f32[512,256]{1,0:T(8,128)S(1)}, f32[512,256]{1,0:T(8,128)}, u32[]{:S(2)}) copy-start(f32[512,256]{1,0:T(8,128)} %param.32) | copy-start | bytes 1572868
  499.8 88.3 %copy-start.14 = (f32[512,256]{1,0:T(8,128)S(1)}, f32[512,256]{1,0:T(8,128)}, u32[]{:S(2)}) copy-start(f32[512,256]{1,0:T(8,128)} %param.30) | copy-start | bytes 1572868
  499.8 139.7 %all-gather.11.cloned.1.call-start = ((), (), s32[]{:S(2)}) async-start(), calls=%async_computation.10 | async-start | bytes 2359296 | tf_op jit(solution)/shard_map/all_gather | solution.py:103
  590.2 173.5 %reduce-scatter.11.cloned.1.call-start = ((), (), s32[]{:S(2)}) async-start(), calls=%async_computation.11 | async-start | bytes 2621440 | tf_op jit(solution)/shard_map/reduce_scatter | solution.py:89
  733.4 1.3 copy-start
  733.4 30.3 %copy-start.5 = (f32[512,256]{1,0:T(8,128)S(1)}, f32[512,256]{1,0:T(8,128)}, u32[]{:S(2)}) copy-start(f32[512,256]{1,0:T(8,128)} %copy-done.4) | copy-start | bytes 1572868
  733.4 30.3 %copy-start.16 = (f32[512,256]{1,0:T(8,128)S(1)}, f32[512,256]{1,0:T(8,128)}, u32[]{:S(2)}) copy-start(f32[512,256]{1,0:T(8,128)} %param.31) | copy-start | bytes 1572868
Sparse Core Ops, SparseCore 0:
  10.1 19.4 all-gather.4
  123.9 86.7 reduce-scatter.4
  213.6 48.7 all-gather.6
  357.2 28.7 reduce-scatter.6
  388.9 16.7 all-gather.8
  499.9 88.0 reduce-scatter.8
  590.8 48.7 all-gather.10
  734.9 28.7 reduce-scatter.10
where the time goes:
time: 775 us; the launch traced here: 772 us
  waiting for transfers between devices  310 us (40%)
  other arithmetic  217 us (28%)
  matrix products  111 us (14%)
  local copies, waits for them, and re-layouts  77.6 us (10%)
  blocking collectives  40.9 us (5%)
  between operations  15 us (2%)
    reduce_scatter x2, waiting for transfers between devices, column_sums(): lax.psum_scatter(partial_value, 'row', scatter_dimension=0, tiled=True)  134 us
    scatter-add x12, other arithmetic, backward_block_step(): return running.at[col_block].add(products)  114 us
    all_gather x2, waiting for transfers between devices, spread(): return lax.all_gather(ahead, 'row', axis=0, tiled=True)  98.1 us
    scatter-add x12, other arithmetic, forward_block_step(): return running.at[row_block].add(products)  73.9 us
    dot_general x12, matrix products, forward_block_step(): jnp.einsum('sij,sjb->sib', tile_block, pieces, preferred_element_type=jnp...  59.4 us
    reduce_scatter x2, waiting for transfers between devices, row_sums(): lax.psum_scatter(forward_part(my_tiles, my_rows, my_cols, slot_count, seg...  57.8 us
    dot_general x12, matrix products, backward_block_step(): jnp.einsum('sij,sib->sjb', tile_block, pieces, preferred_element_type=jnp...  51.9 us
    gather x12, local copies, waits for them, and re-layouts, forward_block_step(): pieces = jnp.take(x_tiles, col_block, axis=0)  43.4 us
  transfers between devices with their start and end apart: 8, of which 8 were waited for; matrix products, arithmetic and copies ran while one was open for 2% of the time, Pallas kernels for 0%

commit v1 on v0

--- a/solution.py
+++ b/solution.py
@@ -6,6 +6,27 @@
 NR_DEV = 8
 SLOT_BLOCK = 16
 eps = 1e-06
+
+
+def joined_along(blocks, dim):
+    shape = list(blocks.shape[1:])
+    shape[dim] *= blocks.shape[0]
+    return jnp.moveaxis(blocks, 0, dim).reshape(shape)
+
+
+def doubled(x, axis):
+    length, index = (lax.axis_size(axis), lax.axis_index(axis))
+    pieces, bit = (x[None], 1)
+    while bit < length:
+        theirs = lax.ppermute(pieces, axis, [(i, i ^ bit) for i in range(length)])
+        low = index & bit == 0
+        pieces = jnp.concatenate([jnp.where(low, pieces, theirs), jnp.where(low, theirs, pieces)])
+        bit *= 2
+    return pieces
+
+
+def collect(x, axis, dim):
+    return joined_along(doubled(x, axis), dim)
 
 
 def forward_part(my_tiles, my_rows, my_cols, slot_count, segment):
@@ -100,7 +121,7 @@
         return lax.psum_scatter(partial_value, "row", scatter_dimension=0, tiled=True)
 
     def spread(ahead):
-        return lax.all_gather(ahead, "row", axis=0, tiled=True)
+        return collect(ahead, "row", 0)
 
     grad_zero = column_sums(dual_rows(y_start))
     primal_one = jnp.clip(x_base - step_primal * (cost_seg - grad_zero), lower_seg, upper_seg)

time: 775 us -> 817 us (1.054)
  waiting for transfers between devices: 310 us -> 335 us
  starting transfers between devices: 0.33 us -> 12.3 us
    ppermute x0 -> x6, waiting for transfers between devices: none -> 122 us  [doubled(): theirs = lax.ppermute(pieces, axis, [(i, i ^ bit) for i in range(length)])]
    all_gather x2 -> x0, waiting for transfers between devices: 98.1 us -> none  [spread(): return lax.all_gather(ahead, 'row', axis=0, tiled=True)]
    ppermute x0 -> x6, starting transfers between devices: none -> 12.1 us  [doubled(): theirs = lax.ppermute(pieces, axis, [(i, i ^ bit) for i in range(length)])]
  transfers between devices with their start and end apart: 8 -> 12, of which waited for: 8 -> 12; matrix products, arithmetic and copies ran while one was open for 2% -> 2% of each run, Pallas kernels for 0% -> 0%
where the time goes in v1:
time: 817 us; the launch traced here: 814 us
  waiting for transfers between devices  335 us (41%)
  other arithmetic  220 us (27%)
  matrix products  112 us (14%)
  local copies, waits for them, and re-layouts  77.8 us (10%)
  blocking collectives  41.2 us (5%)
  between operations  15 us (2%)
  starting transfers between devices  12.3 us (2%)
    reduce_scatter x2, waiting for transfers between devices, column_sums(): lax.psum_scatter(partial_value, 'row', scatter_dimension=0, tiled=True)  134 us
    ppermute x6, waiting for transfers between devices, doubled(): theirs = lax.ppermute(pieces, axis, [(i, i ^ bit) for i in range(length)])  122 us
    scatter-add x12, other arithmetic, backward_block_step(): return running.at[col_block].add(products)  114 us
    scatter-add x12, other arithmetic, forward_block_step(): return running.at[row_block].add(products)  73.9 us
    reduce_scatter x2, waiting for transfers between devices, row_sums(): lax.psum_scatter(forward_part(my_tiles, my_rows, my_cols, slot_count, seg...  59.7 us
    dot_general x12, matrix products, forward_block_step(): jnp.einsum('sij,sjb->sib', tile_block, pieces, preferred_element_type=jnp...  59.6 us
    dot_general x12, matrix products, backward_block_step(): jnp.einsum('sij,sib->sjb', tile_block, pieces, preferred_element_type=jnp...  52.1 us
    gather x12, local copies, waits for them, and re-layouts, forward_block_step(): pieces = jnp.take(x_tiles, col_block, axis=0)  43.5 us
  transfers between devices with their start and end apart: 12, of which 12 were waited for; matrix products, arithmetic and copies ran while one was open for 2% of the time, Pallas kernels for 0%

profile of v1, /device:TPU:0, one launch (start us, length us, event | category | flops | bytes accessed | tf_op | source)
XLA Modules:
  0.0 813.7 jit_solution(17416020310370027735)
XLA Ops:
  9.7 16.7 %copy.14 = bf16[96,256,256]{1,2,0:T(8,128)(2,1)} copy(bf16[96,256,256]{2,1,0:T(8,128)(2,1)} %bitcast.23) | data formatting | bytes 25165824
  32.0 91.9 %while.44 = (s32[]{:T(128)}, f32[16,256,256]{2,1,0:T(8,128)}, s32[]{:T(128)}, s32[96]{0:T(128)S(1)}, s32[]{:T(128)}, /*index=5*/bf16[96,256,256]{1,2,0:T(8,128)(...) while((s32[]{:T(128)}, f32[16,256,256]{2,1,0:T(8,128)}, ...), condition=%wide.region_2.4_spmd.clone, body=%wide.region_0.3_spmd.clone.sunk | while | flops 540017856 | bytes 25170616 | solution.py:77
  37.8 9.6 %scatter_fusion = f32[16,256,256]{2,1,0:T(8,128)} fusion(f32[16,256,256]{2,1,0:T(8,128)} %get-tuple-element.627, s32[16]{0:T(128)S(1)} %compare_select_fusion.16, f32[16,256,256]{2,1,0:T(8,128)} %convolution_select_fusion.8), kind=kCustom, calls=%fused_computation.4.clone.clone.1 | custom fusion | flops 1048576 | bytes 12582976 | tf_op jit(solution)/shard_map/while/body/scatter-add | solution.py:73
  53.2 9.5 %scatter_fusion = f32[16,256,256]{2,1,0:T(8,128)} fusion(f32[16,256,256]{2,1,0:T(8,128)} %get-tuple-element.627, s32[16]{0:T(128)S(1)} %compare_select_fusion.16, f32[16,256,256]{2,1,0:T(8,128)} %convolution_select_fusion.8), kind=kCustom, calls=%fused_computation.4.clone.clone.1 | custom fusion | flops 1048576 | bytes 12582976 | tf_op jit(solution)/shard_map/while/body/scatter-add | solution.py:73
  68.6 9.5 %scatter_fusion = f32[16,256,256]{2,1,0:T(8,128)} fusion(f32[16,256,256]{2,1,0:T(8,128)} %get-tuple-element.627, s32[16]{0:T(128)S(1)} %compare_select_fusion.16, f32[16,256,256]{2,1,0:T(8,128)} %convolution_select_fusion.8), kind=kCustom, calls=%fused_computation.4.clone.clone.1 | custom fusion | flops 1048576 | bytes 12582976 | tf_op jit(solution)/shard_map/while/body/scatter-add | solution.py:73
  83.9 9.5 %scatter_fusion = f32[16,256,256]{2,1,0:T(8,128)} fusion(f32[16,256,256]{2,1,0:T(8,128)} %get-tuple-element.627, s32[16]{0:T(128)S(1)} %compare_select_fusion.16, f32[16,256,256]{2,1,0:T(8,128)} %convolution_select_fusion.8), kind=kCustom, calls=%fused_computation.4.clone.clone.1 | custom fusion | flops 1048576 | bytes 12582976 | tf_op jit(solution)/shard_map/while/body/scatter-add | solution.py:73
  99.2 9.4 %scatter_fusion = f32[16,256,256]{2,1,0:T(8,128)} fusion(f32[16,256,256]{2,1,0:T(8,128)} %get-tuple-element.627, s32[16]{0:T(128)S(1)} %compare_select_fusion.16, f32[16,256,256]{2,1,0:T(8,128)} %convolution_select_fusion.8), kind=kCustom, calls=%fused_computation.4.clone.clone.1 | custom fusion | flops 1048576 | bytes 12582976 | tf_op jit(solution)/shard_map/while/body/scatter-add | solution.py:73
  114.4 9.5 %scatter_fusion = f32[16,256,256]{2,1,0:T(8,128)} fusion(f32[16,256,256]{2,1,0:T(8,128)} %get-tuple-element.627, s32[16]{0:T(128)S(1)} %compare_select_fusion.16, f32[16,256,256]{2,1,0:T(8,128)} %convolution_select_fusion.8), kind=kCustom, calls=%fused_computation.4.clone.clone.1 | custom fusion | flops 1048576 | bytes 12582976 | tf_op jit(solution)/shard_map/while/body/scatter-add | solution.py:73
  124.0 87.0 %reduce-scatter.5.cloned.1.call-done = f32[512,256]{1,0:T(8,128)} async-done(((f32[4096,256]{1,0:T(8,128)}), f32[512,256]{1,0:T(8,128)}) %reduce-scatter.5.cloned.1.call-update) | async-done | bytes 524304 | tf_op jit(solution)/shard_map/reduce_scatter | solution.py:121
  214.7 6.2 collective-permute-done
  222.7 10.7 %collective-permute-done.1 = bf16[2,512,256]{2,1,0:T(8,128)(2,1)S(1)} collective-permute-done((bf16[2,512,256]{2,1,0:T(8,128)(2,1)S(1)}, bf16[2,512,256]{2,1,0:T(8,128)(2,1)S(1)}, u32[]{:S(2)}, u32[]{:S(2)}) %collective-permute-start.1) | collective-permute-done | bytes 524320 | tf_op jit(solution)/shard_map/ppermute | solution.py:21
  236.4 43.9 %collective-permute-done.2 = bf16[4,512,256]{2,1,0:T(8,128)(2,1)S(1)} collective-permute-done((bf16[4,512,256]{2,1,0:T(8,128)(2,1)S(1)}, bf16[4,512,256]{2,1,0:T(8,128)(2,1)S(1)}, u32[]{:S(2)}, u32[]{:S(2)}) %collective-permute-start.2) | collective-permute-done | bytes 1048608 | tf_op jit(solution)/shard_map/ppermute | solution.py:21
  282.1 93.3 %while.45 = (s32[]{:T(128)}, f32[8,256,256]{2,1,0:T(8,128)S(1)}, s32[]{:T(128)}, s32[96]{0:T(128)S(1)}, s32[]{:T(128)}, /*index=5*/bf16[96,256,256]{2,1,0:T(8,12...) while((s32[]{:T(128)}, f32[8,256,256]{2,1,0:T(8,128)S(1)}, ...), condition=%wide.region_6.9_spmd.clone, body=%wide.region_4.8_spmd.clone.sunk | while | flops 540017856 | bytes 25170616 | solution.py:53
  307.0 6.2 scatter_fusion.1
  338.2 6.2 scatter_fusion.1
  376.8 29.8 %reduce-scatter.7.cloned.1.call-done = f32[512,256]{1,0:T(8,128)} async-done(((f32[2048,256]{1,0:T(8,128)}), f32[512,256]{1,0:T(8,128)}) %reduce-scatter.7.cloned.1.call-update) | async-done | bytes 524304 | tf_op jit(solution)/shard_map/reduce_scatter | solution.py:110
  409.4 16.8 %all-gather.5.cloned.1.call-done = bf16[2048,256]{1,0:T(8,128)(2,1)} async-done(((bf16[512,256]{1,0:T(8,128)(2,1)}), bf16[2048,256]{1,0:T(8,128)(2,1)}) %all-gather.5.cloned.1.call-update) | async-done | bytes 1048592 | tf_op jit(solution)/shard_map/all_gather | solution.py:107
  428.6 91.9 %while.46 = (s32[]{:T(128)}, f32[16,256,256]{2,1,0:T(8,128)}, s32[]{:T(128)}, s32[96]{0:T(128)S(1)}, s32[]{:T(128)}, /*index=5*/bf16[96,256,256]{1,2,0:T(8,128)(...) while((s32[]{:T(128)}, f32[16,256,256]{2,1,0:T(8,128)}, ...), condition=%wide.region_14.17_spmd.clone, body=%wide.region_12.16_spmd.clone.sunk | while | flops 540017856 | bytes 25170616 | solution.py:77
  434.5 9.5 %scatter_fusion.2 = f32[16,256,256]{2,1,0:T(8,128)} fusion(f32[16,256,256]{2,1,0:T(8,128)} %get-tuple-element.699, s32[16]{0:T(128)S(1)} %compare_select_fusion.18, f32[16,256,256]{2,1,0:T(8,128)} %convolution_select_fusion.10), kind=kCustom, calls=%fused_computation.6.clone.clone.1 | custom fusion | flops 1048576 | bytes 12582976 | tf_op jit(solution)/shard_map/while/body/scatter-add | solution.py:73
  449.8 9.6 %scatter_fusion.2 = f32[16,256,256]{2,1,0:T(8,128)} fusion(f32[16,256,256]{2,1,0:T(8,128)} %get-tuple-element.699, s32[16]{0:T(128)S(1)} %compare_select_fusion.18, f32[16,256,256]{2,1,0:T(8,128)} %convolution_select_fusion.10), kind=kCustom, calls=%fused_computation.6.clone.clone.1 | custom fusion | flops 1048576 | bytes 12582976 | tf_op jit(solution)/shard_map/while/body/scatter-add | solution.py:73
  465.2 9.5 %scatter_fusion.2 = f32[16,256,256]{2,1,0:T(8,128)} fusion(f32[16,256,256]{2,1,0:T(8,128)} %get-tuple-element.699, s32[16]{0:T(128)S(1)} %compare_select_fusion.18, f32[16,256,256]{2,1,0:T(8,128)} %convolution_select_fusion.10), kind=kCustom, calls=%fused_computation.6.clone.clone.1 | custom fusion | flops 1048576 | bytes 12582976 | tf_op jit(solution)/shard_map/while/body/scatter-add | solution.py:73
  480.6 9.4 %scatter_fusion.2 = f32[16,256,256]{2,1,0:T(8,128)} fusion(f32[16,256,256]{2,1,0:T(8,128)} %get-tuple-element.699, s32[16]{0:T(128)S(1)} %compare_select_fusion.18, f32[16,256,256]{2,1,0:T(8,128)} %convolution_select_fusion.10), kind=kCustom, calls=%fused_computation.6.clone.clone.1 | custom fusion | flops 1048576 | bytes 12582976 | tf_op jit(solution)/shard_map/while/body/scatter-add | solution.py:73
  495.9 9.4 %scatter_fusion.2 = f32[16,256,256]{2,1,0:T(8,128)} fusion(f32[16,256,256]{2,1,0:T(8,128)} %get-tuple-element.699, s32[16]{0:T(128)S(1)} %compare_select_fusion.18, f32[16,256,256]{2,1,0:T(8,128)} %convolution_select_fusion.10), kind=kCustom, calls=%fused_computation.6.clone.clone.1 | custom fusion | flops 1048576 | bytes 12582976 | tf_op jit(solution)/shard_map/while/body/scatter-add | solution.py:73
  511.1 9.5 %scatter_fusion.2 = f32[16,256,256]{2,1,0:T(8,128)} fusion(f32[16,256,256]{2,1,0:T(8,128)} %get-tuple-element.699, s32[16]{0:T(128)S(1)} %compare_select_fusion.18, f32[16,256,256]{2,1,0:T(8,128)} %convolution_select_fusion.10), kind=kCustom, calls=%fused_computation.6.clone.clone.1 | custom fusion | flops 1048576 | bytes 12582976 | tf_op jit(solution)/shard_map/while/body/scatter-add | solution.py:73
  520.7 41.2 %all-reduce = (f32[256]{0:T(256)S(1)}, f32[256]{0:T(256)S(1)}) all-reduce(f32[256]{0:T(256)S(1)} %get-tuple-element.372, f32[256]{0:T(256)S(1)} %get-tuple-element.370), channel_id=1, replica_groups=mesh['row'=8,'col'=4] {'row','col'}, use_global_device_ids=true, to_apply=%region_11.14 | all-reduce | flops 512 | bytes 4096 | tf_op jit(solution)/shard_map/psum | solution.py:134
  561.9 46.9 %reduce-scatter.9.cloned.1.call-done = f32[512,256]{1,0:T(8,128)} async-done(((f32[4096,256]{1,0:T(8,128)}), f32[512,256]{1,0:T(8,128)}) %reduce-scatter.9.cloned.1.call-update) | async-done | bytes 524304 | tf_op jit(solution)/shard_map/reduce_scatter | solution.py:121
  612.3 6.2 collective-permute-done.3
  620.3 10.7 %collective-permute-done.4 = bf16[2,512,256]{2,1,0:T(8,128)(2,1)S(1)} collective-permute-done((bf16[2,512,256]{2,1,0:T(8,128)(2,1)S(1)}, bf16[2,512,256]{2,1,0:T(8,128)(2,1)S(1)}, u32[]{:S(2)}, u32[]{:S(2)}) %collective-permute-start.4) | collective-permute-done | bytes 524320 | tf_op jit(solution)/shard_map/ppermute | solution.py:21
  634.0 43.9 %collective-permute-done.5 = bf16[4,512,256]{2,1,0:T(8,128)(2,1)S(1)} collective-permute-done((bf16[4,512,256]{2,1,0:T(8,128)(2,1)S(1)}, bf16[4,512,256]{2,1,0:T(8,128)(2,1)S(1)}, u32[]{:S(2)}, u32[]{:S(2)}) %collective-permute-start.5) | collective-permute-done | bytes 1048608 | tf_op jit(solution)/shard_map/ppermute | solution.py:21
  679.7 93.8 %while.47 = (s32[]{:T(128)}, f32[8,256,256]{2,1,0:T(8,128)S(1)}, s32[]{:T(128)}, s32[96]{0:T(128)S(1)}, s32[]{:T(128)}, /*index=5*/bf16[96,256,256]{2,1,0:T(8,12...) while((s32[]{:T(128)}, f32[8,256,256]{2,1,0:T(8,128)S(1)}, ...), condition=%wide.region_18.21_spmd.clone, body=%wide.region_16.20_spmd.clone.sunk | while | flops 540017856 | bytes 25170616 | solution.py:53
  704.8 6.2 scatter_fusion.3
  774.9 29.9 %reduce-scatter.11.cloned.1.call-done = f32[512,256]{1,0:T(8,128)} async-done(((f32[2048,256]{1,0:T(8,128)}), f32[512,256]{1,0:T(8,128)}) %reduce-scatter.11.cloned.1.call-update) | async-done | bytes 524304 | tf_op jit(solution)/shard_map/reduce_scatter | solution.py:110
  (217 shorter events, 275.9 us)
Async XLA Ops:
  7.2 22.4 %all-gather.3.cloned.1.call-start = ((), (), s32[]{:S(2)}) async-start(), calls=%async_computation.4 | async-start | bytes 1310720 | tf_op jit(solution)/shard_map/all_gather | solution.py:107
  9.0 202.0 %reduce-scatter.5.cloned.1.call-start = ((), (), s32[]{:S(2)}) async-start(), calls=%async_computation.5 | async-start | bytes 4718592 | tf_op jit(solution)/shard_map/reduce_scatter | solution.py:121
  29.6 2.4 copy-start.2
  29.6 2.4 copy-start.18
  29.6 2.4 copy-start.19
  123.9 87.1 %copy-start.9 = (f32[512,256]{1,0:T(8,128)S(1)}, f32[512,256]{1,0:T(8,128)}, u32[]{:S(2)}) copy-start(f32[512,256]{1,0:T(8,128)} %param.33) | copy-start | bytes 1572868
  123.9 87.1 %copy-start.11 = (f32[512,256]{1,0:T(8,128)S(1)}, f32[512,256]{1,0:T(8,128)}, u32[]{:S(2)}) copy-start(f32[512,256]{1,0:T(8,128)} %param.32) | copy-start | bytes 1572868
  123.9 87.1 %copy-start.13 = (f32[512,256]{1,0:T(8,128)S(1)}, f32[512,256]{1,0:T(8,128)}, u32[]{:S(2)}) copy-start(f32[512,256]{1,0:T(8,128)} %param.30) | copy-start | bytes 1572868
  123.9 87.1 %copy-start.17 = (f32[512,256]{1,0:T(8,128)S(1)}, f32[512,256]{1,0:T(8,128)}, u32[]{:S(2)}) copy-start(f32[512,256]{1,0:T(8,128)} %param.28) | copy-start | bytes 1572868
  123.9 87.1 %copy-start.21 = (f32[256]{0:T(256)S(1)}, f32[256]{0:T(256)}, u32[]{:S(2)}) copy-start(f32[256]{0:T(256)} %param.34) | copy-start | bytes 3076
  123.9 282.7 %reduce-scatter.7.cloned.1.call-start = ((), (), s32[]{:S(2)}) async-start(), calls=%async_computation.6 | async-start | bytes 2621440 | tf_op jit(solution)/shard_map/reduce_scatter | solution.py:110
  213.1 7.7 collective-permute-start
  220.9 12.5 %collective-permute-start.1 = (bf16[2,512,256]{2,1,0:T(8,128)(2,1)S(1)}, bf16[2,512,256]{2,1,0:T(8,128)(2,1)S(1)}, u32[]{:S(2)}, u32[]{:S(2)}) collective-permute-start(bf16[2,512,256]{2,1,0:T(8,128)(2,1)S(1)} %pad_maximum_fusion.4), channel_id=1, source_target_pairs={{0,8},{4,12},{8,0},{12,4},{16,24},{20,28},{24,16},{28,20},{1,9},{5... | collective-permute-start | bytes 1572872 | tf_op jit(solution)/shard_map/ppermute | solution.py:21
  233.6 46.6 %collective-permute-start.2 = (bf16[4,512,256]{2,1,0:T(8,128)(2,1)S(1)}, bf16[4,512,256]{2,1,0:T(8,128)(2,1)S(1)}, u32[]{:S(2)}, u32[]{:S(2)}) collective-permute-start(bf16[4,512,256]{2,1,0:T(8,128)(2,1)S(1)} %pad_maximum_fusion.2), channel_id=1, source_target_pairs={{0,16},{4,20},{8,24},{12,28},{16,0},{20,4},{24,8},{28,12},{1,17},{... | collective-permute-start | bytes 3145736 | tf_op jit(solution)/shard_map/ppermute | solution.py:21
  375.5 1.3 copy-start.1
  375.5 31.2 %copy-start.8 = (f32[512,256]{1,0:T(8,128)S(1)}, f32[512,256]{1,0:T(8,128)}, u32[]{:S(2)}) copy-start(f32[512,256]{1,0:T(8,128)} %param.29) | copy-start | bytes 1572868
  375.5 31.2 %copy-start.15 = (f32[512,256]{1,0:T(8,128)S(1)}, f32[512,256]{1,0:T(8,128)}, u32[]{:S(2)}) copy-start(f32[512,256]{1,0:T(8,128)} %param.31) | copy-start | bytes 1572868
  375.5 31.2 %copy-start.20 = (f32[256]{0:T(256)S(1)}, f32[256]{0:T(256)}, u32[]{:S(2)}) copy-start(f32[256]{0:T(256)} %param.35) | copy-start | bytes 3076
  376.8 49.5 %all-gather.5.cloned.1.call-start = ((), (), s32[]{:S(2)}) async-start(), calls=%async_computation.7 | async-start | bytes 1310720 | tf_op jit(solution)/shard_map/all_gather | solution.py:107
  409.4 199.4 %reduce-scatter.9.cloned.1.call-start = ((), (), s32[]{:S(2)}) async-start(), calls=%async_computation.8 | async-start | bytes 4718592 | tf_op jit(solution)/shard_map/reduce_scatter | solution.py:121
  426.3 2.4 copy-start.3
  520.6 88.2 %copy-start.5 = (f32[512,256]{1,0:T(8,128)S(1)}, f32[512,256]{1,0:T(8,128)}, u32[]{:S(2)}) copy-start(f32[512,256]{1,0:T(8,128)} %copy-done.4) | copy-start | bytes 1572868
  520.6 88.2 %copy-start.10 = (f32[512,256]{1,0:T(8,128)S(1)}, f32[512,256]{1,0:T(8,128)}, u32[]{:S(2)}) copy-start(f32[512,256]{1,0:T(8,128)} %param.33) | copy-start | bytes 1572868
  520.6 88.2 %copy-start.12 = (f32[512,256]{1,0:T(8,128)S(1)}, f32[512,256]{1,0:T(8,128)}, u32[]{:S(2)}) copy-start(f32[512,256]{1,0:T(8,128)} %param.32) | copy-start | bytes 1572868
  520.6 88.2 %copy-start.14 = (f32[512,256]{1,0:T(8,128)S(1)}, f32[512,256]{1,0:T(8,128)}, u32[]{:S(2)}) copy-start(f32[512,256]{1,0:T(8,128)} %param.30) | copy-start | bytes 1572868
  520.6 284.3 %reduce-scatter.11.cloned.1.call-start = ((), (), s32[]{:S(2)}) async-start(), calls=%async_computation.9 | async-start | bytes 2621440 | tf_op jit(solution)/shard_map/reduce_scatter | solution.py:110
  610.8 7.7 collective-permute-start.3
  618.6 12.5 %collective-permute-start.4 = (bf16[2,512,256]{2,1,0:T(8,128)(2,1)S(1)}, bf16[2,512,256]{2,1,0:T(8,128)(2,1)S(1)}, u32[]{:S(2)}, u32[]{:S(2)}) collective-permute-start(bf16[2,512,256]{2,1,0:T(8,128)(2,1)S(1)} %pad_maximum_fusion.5), channel_id=1, source_target_pairs={{0,8},{4,12},{8,0},{12,4},{16,24},{20,28},{24,16},{28,20},{1,9},{5... | collective-permute-start | bytes 1572872 | tf_op jit(solution)/shard_map/ppermute | solution.py:21
  631.2 46.6 %collective-permute-start.5 = (bf16[4,512,256]{2,1,0:T(8,128)(2,1)S(1)}, bf16[4,512,256]{2,1,0:T(8,128)(2,1)S(1)}, u32[]{:S(2)}, u32[]{:S(2)}) collective-permute-start(bf16[4,512,256]{2,1,0:T(8,128)(2,1)S(1)} %pad_maximum_fusion.3), channel_id=1, source_target_pairs={{0,16},{4,20},{8,24},{12,28},{16,0},{20,4},{24,8},{28,12},{1,17},{... | collective-permute-start | bytes 3145736 | tf_op jit(solution)/shard_map/ppermute | solution.py:21
  773.6 1.4 copy-start
  773.6 31.3 %copy-start.7 = (f32[512,256]{1,0:T(8,128)S(1)}, f32[512,256]{1,0:T(8,128)}, u32[]{:S(2)}) copy-start(f32[512,256]{1,0:T(8,128)} %copy-done.6) | copy-start | bytes 1572868
  773.6 31.3 %copy-start.16 = (f32[512,256]{1,0:T(8,128)S(1)}, f32[512,256]{1,0:T(8,128)}, u32[]{:S(2)}) copy-start(f32[512,256]{1,0:T(8,128)} %param.31) | copy-start | bytes 1572868
  (2 other events, 1.6 us)
Sparse Core Ops, SparseCore 0:
  10.1 19.4 all-gather.2
  124.1 86.9 reduce-scatter.4
  376.9 29.6 reduce-scatter.6
  409.5 16.6 all-gather.4
  520.7 87.9 reduce-scatter.8
  775.1 29.7 reduce-scatter.10
